TPU v7x, 32 devices: a whole 2x2x4 slice. The times are simulated.
32 devices in a mesh: row: 4 (over y, core), col: 8 (over z, x).
Axes of the slice: x: 2, y: 2, z: 4, core: 2. Of those that a mesh axis runs over, the one named last changes fastest.
Arguments:
- sources: bfloat16 [4, 8, 4, 256, 256], P('row', 'col'), may hold values from -6 to 6
- history: bfloat16 [4, 8, 8, 256, 256], P(None, 'col'), may hold values from -4 to 4
- inverse_diagonal: float32 [4, 8, 256], P('row', 'col'), may hold values from 0.3 to 0.6
- far_cores: bfloat16 [4, 8, 32, 4, 8, 8, 32], P('row', None, None, None, 'col'), may hold values from -0.09375 to 0.09375
- target_basis: bfloat16 [4, 8, 256, 32], P('row', 'col'), may hold values from -1 to 1
- source_basis: bfloat16 [4, 8, 256, 32], P(None, 'col'), may hold values from -0.375 to 0.375
- near_blocks: bfloat16 [4, 8, 3, 256, 8, 256], P('row', 'col'), may hold values from -0.078125 to 0.078125
- near_tile: int32 [4, 8, 3], P('row', 'col'), may hold values from 0 to 3
- near_count: int32 [4, 8], P('row', 'col'), may hold values from 1 to 3, as said below
Outputs:
- new_steps: bfloat16 [4, 8, 4, 256, 256], P('row', 'col')
- energies: float32 [4, 256], replicated
Inputs may be any that keep to these rules, and one draw needn't show every extreme that they name: Only slots below near_count are used; in every draw some tile has all 3 slots live.
All inputs are finite; a program needn't handle non-finite values.
Results may differ from a plain program's by a relative error of at most 0.011.
Values may be sent and summed in bfloat16 or wider, within the bound.
A program may use at most 192 MiB of HBM per device.

v0:
```python
import jax
import jax.numpy as jnp
from jax import lax
from jax.sharding import PartitionSpec as P


def local(
    sources,
    history,
    inverse_diagonal,
    far_cores,
    target_basis,
    source_basis,
    near_blocks,
    near_tile,
    near_count,
):
    row_count = history.shape[0]
    col_count = far_cores.shape[1]
    rank_size = far_cores.shape[2]
    lag_count = history.shape[2]
    tile_size = history.shape[3]
    field_count = history.shape[4]
    step_count = sources.shape[2]
    panel_total = row_count * col_count * tile_size
    column_past = history[:, 0]
    basis = source_basis[:, 0]
    projected = jnp.einsum(
        "pta,pktx->pkax", basis, column_past, preferred_element_type=jnp.float32
    ).astype(jnp.bfloat16)
    core_matrix = far_cores.reshape(col_count * rank_size, row_count * lag_count * rank_size)
    own_basis = target_basis[0, 0]
    scaling = inverse_diagonal[0, 0][:, None]
    blocks_here = near_blocks[0, 0]
    tiles_here = near_tile[0, 0]
    live_count = near_count[0, 0]
    outputs = []
    energy_rows = []
    for moment in range(step_count):
        partial_value = jnp.dot(
            core_matrix,
            projected.reshape(row_count * lag_count * rank_size, field_count),
            preferred_element_type=jnp.float32,
        )

        def add_block(slot, total):
            source = lax.dynamic_index_in_dim(
                column_past, tiles_here[slot], 0, keepdims=False
            ).reshape(lag_count * tile_size, field_count)
            block = lax.dynamic_index_in_dim(blocks_here, slot, 0, keepdims=False).reshape(
                tile_size, lag_count * tile_size
            )
            return total + jnp.dot(block, source, preferred_element_type=jnp.float32)

        near = lax.fori_loop(
            0, live_count, add_block, jnp.zeros((tile_size, field_count), jnp.float32)
        )
        own_core = lax.psum_scatter(
            partial_value.astype(jnp.bfloat16), "col", scatter_dimension=0, tiled=True
        )
        far = jnp.dot(own_basis, own_core, preferred_element_type=jnp.float32)
        fresh = (scaling * (sources[0, 0, moment].astype(jnp.float32) - far - near)).astype(
            jnp.bfloat16
        )
        outputs.append(fresh)
        squares = jnp.sum(jnp.square(fresh.astype(jnp.float32)), axis=0) / panel_total
        energy_rows.append(lax.psum(squares, ("row", "col")))
        if moment + 1 < step_count:
            gathered = lax.all_gather(fresh[None], "row", axis=0, tiled=True)
            column_past = jnp.concatenate([gathered[:, None], column_past[:, :-1]], axis=1)
            fresh_proj = jnp.einsum(
                "pta,ptx->pax", basis, gathered, preferred_element_type=jnp.float32
            ).astype(jnp.bfloat16)
            projected = jnp.concatenate([fresh_proj[:, None], projected[:, :-1]], axis=1)
    energies = jnp.stack(energy_rows, axis=0)
    new_steps = jnp.stack(outputs, axis=0)[None, None]
    return (new_steps, energies)


def solution(mesh):
    placed = (
        P("row", "col", None, None, None),
        P(None, "col", None, None, None),
        P("row", "col", None),
        P("row", None, None, None, "col", None, None),
        P("row", "col", None, None),
        P(None, "col", None, None),
        P("row", "col", None, None, None, None),
        P("row", "col", None),
        P("row", "col"),
    )
    return jax.shard_map(
        local,
        mesh=mesh,
        in_specs=placed,
        out_specs=(P("row", "col", None, None, None), P()),
        check_vma=False,
    )
```

profile of v0, /device:TPU:0, one launch (start us, length us, event | category | flops | bytes accessed | tf_op | source)
XLA Modules:
  0.0 396.4 jit_solution(5392760271177488294)
XLA Ops:
  7.2 3.5 reshape.69
  10.8 3.2 convolution_convert_fusion
  14.4 0.8 copy.20
  15.2 2.6 copy.29
  17.9 14.3 %while.40 = (s32[]{:T(128)}, f32[256,256]{1,0:T(8,128)S(1)}, s32[]{:T(128)}, bf16[3,256,8,256]{3,1,2,0:T(8,128)(2,1)S(1)}, s32[3]{0:T(128)S(1)}, /*index=5*/bf16...) while((s32[]{:T(128)}, f32[256,256]{1,0:T(8,128)S(1)}, s32[]{:T(128)}, ...), condition=%wide.region_2.3_spmd, body=%wide.region_1.2_spmd.sunk | while | flops 268500992 | bytes 2621629 | solution.py:55
  20.7 1.7 fusion.89
  25.3 1.7 fusion.89
  29.9 1.7 fusion.89
  32.2 4.3 %slice.41 = bf16[4,7,256,256]{3,2,1,0:T(8,128)(2,1)} slice(bf16[4,8,256,256]{3,2,1,0:T(8,128)(2,1)} %get-tuple-element.477), slice={[0:4], [0:7], [0:256], [0:256]} | slice | bytes 7340032 | tf_op jit(solution)/shard_map/slice | solution.py:70
  36.5 1.9 slice.40
  38.4 41.5 %reduce-scatter.13.cloned.1.call-done = bf16[32,256]{1,0:T(8,128)(2,1)} async-done(((bf16[256,256]{1,0:T(8,128)(2,1)}), bf16[32,256]{1,0:T(8,128)(2,1)}) %reduce-scatter.13.cloned.1.call-update) | async-done | bytes 16400
  79.9 1.7 multiply_reduce_fusion.3
  81.6 0.6 copy-done.6
  82.3 7.1 %all-gather = bf16[1024,256]{1,0:T(8,128)(2,1)S(1)} all-gather(bf16[256,256]{1,0:T(8,128)(2,1)S(1)} %get-tuple-element.197), channel_id=2, replica_groups=mesh['row'=4,'col'=8] {'row'}, dimensions={0}, use_global_device_ids=true | all-gather | bytes 655360 | tf_op jit(solution)/shard_map/all_gather | solution.py:69
  89.4 4.5 %pad_maximum_fusion = bf16[4,8,256,256]{3,2,1,0:T(8,128)(2,1)} fusion(bf16[4,1,256,256]{3,2,1,0:T(8,128)(2,1)S(1)} %bitcast.237, bf16[4,7,256,256]{3,2,1,0:T(8,128)(2,1)} %slice.41), kind=kLoop, calls=%fused_computation.29 | loop fusion | flops 2097152 | bytes 8388608 | tf_op jit(solution)/shard_map/concatenate | solution.py:70
  94.0 15.9 %while.41 = (s32[]{:T(128)}, f32[256,256]{1,0:T(8,128)S(1)}, s32[]{:T(128)}, bf16[3,256,8,256]{3,1,2,0:T(8,128)(2,1)S(1)}, s32[3]{0:T(128)S(1)}, /*index=5*/bf16...) while((s32[]{:T(128)}, f32[256,256]{1,0:T(8,128)S(1)}, s32[]{:T(128)}, ...), condition=%wide.region_5.6_spmd, body=%wide.region_4.5_spmd.sunk | while | flops 268500992 | bytes 2621629 | solution.py:55
  94.6 0.7 dynamic_slice.87
  97.4 1.7 fusion.92
  99.7 0.7 dynamic_slice.87
  102.5 1.7 fusion.92
  104.8 0.7 dynamic_slice.87
  107.6 1.7 fusion.92
  110.4 1.2 fusion.46
  111.6 1.1 pad_maximum_fusion.3
  112.7 2.0 fusion.43
  114.8 1.7 copy.22
  116.5 1.2 broadcast_multiply_fusion.3
  117.7 1.8 fusion.50
  119.5 3.5 fusion.25
  123.0 53.8 %reduce-scatter.15.cloned.1.call-done = bf16[32,256]{1,0:T(8,128)(2,1)} async-done(((bf16[256,256]{1,0:T(8,128)(2,1)}), bf16[32,256]{1,0:T(8,128)(2,1)}) %reduce-scatter.15.cloned.1.call-update) | async-done | bytes 16400
  176.8 1.7 multiply_reduce_fusion.2
  178.5 0.6 copy-done.7
  179.2 7.1 %all-gather.1 = bf16[1024,256]{1,0:T(8,128)(2,1)S(1)} all-gather(bf16[256,256]{1,0:T(8,128)(2,1)S(1)} %get-tuple-element.195), channel_id=3, replica_groups=mesh['row'=4,'col'=8] {'row'}, dimensions={0}, use_global_device_ids=true | all-gather | bytes 655360 | tf_op jit(solution)/shard_map/all_gather | solution.py:69
  186.3 4.5 %pad_maximum_fusion.1 = bf16[4,8,256,256]{3,2,1,0:T(8,128)(2,1)} fusion(bf16[4,1,256,256]{3,2,1,0:T(8,128)(2,1)S(1)} %bitcast.240, bf16[4,7,256,256]{3,2,1,0:T(8,128)(2,1)} %fusion.25), kind=kLoop, calls=%fused_computation.31 | loop fusion | flops 2097152 | bytes 8388608 | tf_op jit(solution)/shard_map/concatenate | solution.py:70
  190.9 15.8 %while.42 = (s32[]{:T(128)}, f32[256,256]{1,0:T(8,128)S(1)}, s32[]{:T(128)}, bf16[3,256,8,256]{3,1,2,0:T(8,128)(2,1)S(1)}, s32[3]{0:T(128)S(1)}, /*index=5*/bf16...) while((s32[]{:T(128)}, f32[256,256]{1,0:T(8,128)S(1)}, s32[]{:T(128)}, ...), condition=%wide.region_8.9_spmd, body=%wide.region_7.8_spmd.sunk | while | flops 268500992 | bytes 2621629 | solution.py:55
  191.5 0.7 dynamic_slice.90
  194.2 1.7 fusion.95
  196.6 0.7 dynamic_slice.90
  199.3 1.7 fusion.95
  201.6 0.7 dynamic_slice.90
  204.3 1.7 fusion.95
  206.6 1.2 fusion.47
  207.9 1.1 pad_maximum_fusion.4
  209.0 2.0 fusion.44
  211.0 1.7 copy.24
  212.7 1.2 broadcast_multiply_fusion.2
  214.0 1.8 fusion.49
  215.8 3.4 fusion.24
  219.2 53.8 %reduce-scatter.17.cloned.1.call-done = bf16[32,256]{1,0:T(8,128)(2,1)} async-done(((bf16[256,256]{1,0:T(8,128)(2,1)}), bf16[32,256]{1,0:T(8,128)(2,1)}) %reduce-scatter.17.cloned.1.call-update) | async-done | bytes 16400
  273.0 1.2 multiply_reduce_fusion.1
  274.2 7.1 %all-gather.2 = bf16[1024,256]{1,0:T(8,128)(2,1)S(1)} all-gather(bf16[256,256]{1,0:T(8,128)(2,1)S(1)} %get-tuple-element.193), channel_id=4, replica_groups=mesh['row'=4,'col'=8] {'row'}, dimensions={0}, use_global_device_ids=true | all-gather | bytes 655360 | tf_op jit(solution)/shard_map/all_gather | solution.py:69
  281.4 0.8 copy-done.5
  282.4 1.1 pad_maximum_fusion.5
  283.4 1.4 fusion.45
  284.8 0.8 copy.26
  285.6 4.5 %pad_maximum_fusion.2 = bf16[4,8,256,256]{3,2,1,0:T(8,128)(2,1)} fusion(bf16[4,7,256,256]{3,2,1,0:T(8,128)(2,1)} %fusion.24, bf16[4,1,256,256]{3,2,1,0:T(8,128)(2,1)} %bitcast.246), kind=kLoop, calls=%fused_computation.32 | loop fusion | flops 2097152 | bytes 8388608 | tf_op jit(solution)/shard_map/concatenate | solution.py:70
  290.1 15.3 %while.43 = (s32[]{:T(128)}, f32[256,256]{1,0:T(8,128)S(1)}, s32[]{:T(128)}, bf16[3,256,8,256]{3,1,2,0:T(8,128)(2,1)S(1)}, s32[3]{0:T(128)S(1)}, /*index=5*/bf16...) while((s32[]{:T(128)}, f32[256,256]{1,0:T(8,128)S(1)}, s32[]{:T(128)}, ...), condition=%wide.region_11.12_spmd, body=%wide.region_10.11_spmd.sunk | while | flops 268500992 | bytes 2621629 | solution.py:55
  293.3 1.7 fusion.98
  298.2 1.7 fusion.98
  303.1 1.7 fusion.98
  305.5 40.5 %reduce-scatter.19.cloned.1.call-done = bf16[32,256]{1,0:T(8,128)(2,1)} async-done(((bf16[256,256]{1,0:T(8,128)(2,1)}), bf16[32,256]{1,0:T(8,128)(2,1)}) %reduce-scatter.19.cloned.1.call-update) | async-done | bytes 16400
  346.0 1.2 multiply_reduce_fusion
  347.2 40.1 %all-reduce = (f32[1,256]{1,0:T(1,128)S(1)}, f32[1,256]{1,0:T(1,128)S(1)}, f32[1,256]{1,0:T(1,128)S(1)}, f32[1,256]{1,0:T(1,128)S(1)}) all-reduce(f32[1,256]{1,0:T(1,128)S(1)} %bitcast.261, f32[1,256]{1,0:T(1,128)S(1)} %bitcast.260, f32[1,256]{1,0:T(1,128)S(1)} %bitcast.259, ...), channel_id=1, replica_groups=mesh['row'=4,'col'=8] {'row','col'}, use_global_device_ids=true, to_apply=%region_19.20 | all-reduce | flops 1024 | bytes 8192 | tf_op jit(solution)/shard_map/psum | solution.py:67
  388.0 1.9 maximum_bitcast_fusion
  (58 shorter events, 5.5 us)
Async XLA Ops:
  7.2 3.6 copy-start
  7.2 72.7 %reduce-scatter.13.cloned.1.call-start = ((), (), s32[]{:S(2)}) async-start(), calls=%async_computation.4 | async-start | bytes 147456
  10.8 4.4 %copy-start.1 = (bf16[256,1024]{1,0:T(8,128)(2,1)}, bf16[256,1024]{1,0:T(8,128)(2,1)S(1)}, u32[]{:S(2)}) copy-start(bf16[256,1024]{1,0:T(8,128)(2,1)S(1)} %reshape.69) | copy-start | bytes 1572868
  14.0 1.2 copy-start.4
  14.0 3.9 copy-start.15
  15.2 161.6 %reduce-scatter.15.cloned.1.call-start = ((), (), s32[]{:S(2)}) async-start(), calls=%async_computation.5 | async-start | bytes 147456
  32.2 47.6 %copy-start.9 = (bf16[1,1,256,32]{2,3,1,0:T(8,128)(2,1)S(1)}, bf16[1,1,256,32]{2,3,1,0:T(8,128)(2,1)}, u32[]{:S(2)}) copy-start(bf16[1,1,256,32]{2,3,1,0:T(8,128)(2,1)} %param.21) | copy-start | bytes 49156
  32.2 47.6 %copy-start.10 = (f32[1,1,256]{2,1,0:T(1,128)S(1)}, f32[1,1,256]{2,1,0:T(1,128)}, u32[]{:S(2)}) copy-start(f32[1,1,256]{2,1,0:T(1,128)} %param.19) | copy-start | bytes 3076
  81.6 0.6 copy-start.6
  89.4 4.5 %copy-start.2 = (bf16[1024,256]{1,0:T(8,128)(2,1)}, bf16[1024,256]{1,0:T(8,128)(2,1)S(1)}, u32[]{:S(2)}) copy-start(bf16[1024,256]{1,0:T(8,128)(2,1)S(1)} %all-gather) | copy-start | bytes 1572868
  109.9 0.5 copy-start.16
  116.4 156.6 %reduce-scatter.17.cloned.1.call-start = ((), (), s32[]{:S(2)}) async-start(), calls=%async_computation.6 | async-start | bytes 147456
  119.5 57.3 %copy-start.11 = (f32[1,1,256]{2,1,0:T(1,128)S(1)}, f32[1,1,256]{2,1,0:T(1,128)}, u32[]{:S(2)}) copy-start(f32[1,1,256]{2,1,0:T(1,128)} %param.19) | copy-start | bytes 3076
  178.5 0.6 copy-start.7
  186.3 4.5 %copy-start.3 = (bf16[1024,256]{1,0:T(8,128)(2,1)}, bf16[1024,256]{1,0:T(8,128)(2,1)S(1)}, u32[]{:S(2)}) copy-start(bf16[1024,256]{1,0:T(8,128)(2,1)S(1)} %all-gather.1) | copy-start | bytes 1572868
  186.3 4.6 %copy-start.17 = (s32[3]{0:T(128)S(1)}, s32[3]{0:T(128)}, u32[]{:S(2)}) copy-start(s32[3]{0:T(128)} %copy-done.16) | copy-start | bytes 40
  212.7 133.3 %reduce-scatter.19.cloned.1.call-start = ((), (), s32[]{:S(2)}) async-start(), calls=%async_computation.7 | async-start | bytes 147456
  215.8 57.2 %copy-start.12 = (f32[1,1,256]{2,1,0:T(1,128)S(1)}, f32[1,1,256]{2,1,0:T(1,128)}, u32[]{:S(2)}) copy-start(f32[1,1,256]{2,1,0:T(1,128)} %param.19) | copy-start | bytes 3076
  274.2 7.2 %copy-start.8 = (bf16[256,256]{1,0:T(8,128)(2,1)}, bf16[256,256]{1,0:T(8,128)(2,1)S(1)}, u32[]{:S(2)}) copy-start(bf16[256,256]{1,0:T(8,128)(2,1)S(1)} %get-tuple-element.193) | copy-start | bytes 393220
  281.4 0.8 copy-start.5
  285.6 4.5 %copy-start.18 = (s32[3]{0:T(128)S(1)}, s32[3]{0:T(128)}, u32[]{:S(2)}) copy-start(s32[3]{0:T(128)} %copy-done.16) | copy-start | bytes 40
  290.1 57.1 %copy-start.13 = (f32[256]{0:T(256)S(1)}, f32[256]{0:T(256)}, u32[]{:S(2)}) copy-start(f32[256]{0:T(256)} %broadcast_multiply_fusion.3) | copy-start | bytes 3076
  290.1 57.1 %copy-start.14 = (f32[256]{0:T(256)S(1)}, f32[256]{0:T(256)}, u32[]{:S(2)}) copy-start(f32[256]{0:T(256)} %broadcast_multiply_fusion.2) | copy-start | bytes 3076
Sparse Core Ops, SparseCore 0:
  15.3 64.5 reduce-scatter.12
  116.6 60.1 reduce-scatter.14
  212.8 60.1 reduce-scatter.16
  285.7 60.2 reduce-scatter.18
where the time goes:
time: 398 us; the launch traced here: 396 us
  waiting for transfers between devices  190 us (48%)
  blocking collectives  61.5 us (15%)
  matrix products  37.7 us (9%)
  loops' own time  33.8 us (8%)
  other arithmetic  32.2 us (8%)
  local copies, waits for them, and re-layouts  27.2 us (7%)
  between operations  14 us (4%)
    unnamed x8, waiting for transfers between devices  190 us
    psum x1, blocking collectives, local(): energy_rows.append(lax.psum(squares, ('row', 'col')))  40.1 us
    another operation x4, loops' own time, local(): lax.fori_loop(0, live_count, add_block, jnp.zeros((tile_size, field_count...  33.8 us
    all_gather x3, blocking collectives, local(): gathered = lax.all_gather(fresh[None], 'row', axis=0, tiled=True)  21.4 us
    concatenate x5, other arithmetic, local(): jnp.concatenate([gathered[:, None], column_past[:, :-1]], axis=1)  20.4 us
    dot_general x12, matrix products, add_block(): return total + jnp.dot(block, source, preferred_element_type=jnp.float32)  20.1 us
    unnamed x43, local copies, waits for them, and re-layouts  10.1 us
  transfers between devices with their start and end apart: 4, of which 4 were waited for; matrix products, arithmetic and copies ran while one was open for 10% of the time, Pallas kernels for 0%

commit v1 on v0

--- a/solution.py
+++ b/solution.py
@@ -66,7 +66,17 @@
         squares = jnp.sum(jnp.square(fresh.astype(jnp.float32)), axis=0) / panel_total
         energy_rows.append(lax.psum(squares, ("row", "col")))
         if moment + 1 < step_count:
-            gathered = lax.all_gather(fresh[None], "row", axis=0, tiled=True)
+            arr = fresh[None]
+            size_here = lax.psum(1, axis_name="row")
+            step_out = arr
+            leaves = [step_out]
+            p_next = sorted(((num, (num + 1) % size_here) for num in range(size_here)))
+            for d in range(1, size_here):
+                step_out = lax.ppermute(step_out, axis_name="row", perm=p_next)
+                leaves.insert(0, step_out)
+            gathered = jnp.roll(
+                jnp.concatenate(leaves, 0), (lax.axis_index("row") + 1) * arr.shape[0], 0
+            )
             column_past = jnp.concatenate([gathered[:, None], column_past[:, :-1]], axis=1)
             fresh_proj = jnp.einsum(
                 "pta,ptx->pax", basis, gathered, preferred_element_type=jnp.float32

time: 398 us -> 372 us (0.935)
  blocking collectives: 61.5 us -> 40.1 us
  waiting for transfers between devices: 190 us -> 186 us
    unnamed x8, waiting for transfers between devices: 190 us -> 161 us
    ppermute x0 -> x9, waiting for transfers between devices: none -> 25 us  [local(): step_out = lax.ppermute(step_out, axis_name='row', perm=p_next)]
    all_gather x3 -> x0, blocking collectives: 21.4 us -> none  [local(): gathered = lax.all_gather(fresh[None], 'row', axis=0, tiled=True)]
    concatenate x5, other arithmetic: 6.86 us -> 0.23 us  [local(): jnp.concatenate([fresh_proj[:, None], projected[:, :-1]], axis=1)]
    broadcast_in_dim x0 -> x3, other arithmetic: none -> 5.28 us  [local(): gathered[:, None]]
    dot_general x4, matrix products: 5.82 us -> 1.39 us  [local(): jnp.dot(core_matrix, projected.reshape(row_count * lag_count * rank_size,...]
    unnamed x43 -> x59, local copies, waits for them, and re-layouts: 10.1 us -> 7.08 us
  transfers between devices with their start and end apart: 4 -> 13, of which waited for: 4 -> 12; matrix products, arithmetic and copies ran while one was open for 10% -> 19% of each run, Pallas kernels for 0% -> 0%
where the time goes in v1:
time: 372 us; the launch traced here: 370 us
  waiting for transfers between devices  186 us (50%)
  blocking collectives  40.1 us (11%)
  matrix products  35.4 us (10%)
  loops' own time  33.6 us (9%)
  other arithmetic  31.1 us (8%)
  local copies, waits for them, and re-layouts  27.9 us (8%)
  between operations  14.2 us (4%)
    unnamed x8, waiting for transfers between devices  161 us
    psum x1, blocking collectives, local(): energy_rows.append(lax.psum(squares, ('row', 'col')))  40.1 us
    another operation x4, loops' own time, local(): lax.fori_loop(0, live_count, add_block, jnp.zeros((tile_size, field_count...  33.6 us
    ppermute x9, waiting for transfers between devices, local(): step_out = lax.ppermute(step_out, axis_name='row', perm=p_next)  25 us
    concatenate x5, other arithmetic, local(): jnp.concatenate([gathered[:, None], column_past[:, :-1]], axis=1)  20.6 us
    dot_general x12, matrix products, add_block(): return total + jnp.dot(block, source, preferred_element_type=jnp.float32)  20.1 us
    dynamic_slice x12, local copies, waits for them, and re-layouts, add_block(): tiles_here[slot]  11.2 us
  transfers between devices with their start and end apart: 13, of which 12 were waited for; matrix products, arithmetic and copies ran while one was open for 19% of the time, Pallas kernels for 0%

profile of v1, /device:TPU:0, one launch (start us, length us, event | category | flops | bytes accessed | tf_op | source)
XLA Modules:
  0.0 369.7 jit_solution(4966316577009945899)
XLA Ops:
  7.2 3.5 reshape.69
  10.8 3.2 convolution_convert_fusion
  14.4 0.8 copy.14
  15.2 2.6 copy.23
  17.9 15.2 %while.40 = (s32[]{:T(128)}, f32[256,256]{1,0:T(8,128)S(1)}, s32[]{:T(128)}, bf16[3,256,8,256]{3,1,2,0:T(8,128)(2,1)S(1)}, s32[3]{0:T(128)S(1)}, /*index=5*/bf16...) while((s32[]{:T(128)}, f32[256,256]{1,0:T(8,128)S(1)}, s32[]{:T(128)}, ...), condition=%wide.region_2.3_spmd, body=%wide.region_1.2_spmd.sunk | while | flops 268500992 | bytes 2621629 | solution.py:55
  21.1 1.7 fusion.116
  25.9 1.7 fusion.116
  30.8 1.7 fusion.116
  33.1 46.7 %reduce-scatter.13.cloned.1.call-done = bf16[32,256]{1,0:T(8,128)(2,1)} async-done(((bf16[256,256]{1,0:T(8,128)(2,1)}), bf16[32,256]{1,0:T(8,128)(2,1)}) %reduce-scatter.13.cloned.1.call-update) | async-done | bytes 16400
  79.8 1.7 multiply_reduce_fusion.3
  82.2 4.4 %collective-permute-done = bf16[1,256,256]{2,1,0:T(8,128)(2,1)S(1)} collective-permute-done((bf16[1,256,256]{2,1,0:T(8,128)(2,1)S(1)}, bf16[1,256,256]{2,1,0:T(8,128)(2,1)S(1)}, u32[]{:S(2)}, u32[]{:S(2)}) %collective-permute-start) | collective-permute-done | bytes 131104 | tf_op jit(solution)/shard_map/ppermute | solution.py:75
  86.6 4.5 %collective-permute-done.1 = bf16[1,256,256]{2,1,0:T(8,128)(2,1)} collective-permute-done((bf16[1,256,256]{2,1,0:T(8,128)(2,1)S(1)}, bf16[1,256,256]{2,1,0:T(8,128)(2,1)}, u32[]{:S(2)}, u32[]{:S(2)}) %collective-permute-start.1) | collective-permute-done | bytes 131104 | tf_op jit(solution)/shard_map/ppermute | solution.py:75
  91.1 4.2 %slice.41 = bf16[4,7,256,256]{3,2,1,0:T(8,128)(2,1)} slice(bf16[4,8,256,256]{3,2,1,0:T(8,128)(2,1)} %get-tuple-element.478), slice={[0:4], [0:7], [0:256], [0:256]} | slice | bytes 7340032 | tf_op jit(solution)/shard_map/slice | solution.py:80
  95.4 1.8 slice.40
  97.2 1.8 fusion.46
  99.4 0.8 copy.16
  100.3 1.8 fusion.98
  102.0 4.6 %pad_maximum_fusion = bf16[4,8,256,256]{3,2,1,0:T(8,128)(2,1)} fusion(bf16[4,1,256,256]{3,2,1,0:T(8,128)(2,1)S(1)} %fusion.98, bf16[4,7,256,256]{3,2,1,0:T(8,128)(2,1)} %slice.41), kind=kLoop, calls=%fused_computation.29 | loop fusion | flops 2097152 | bytes 8388608 | tf_op jit(solution)/shard_map/concatenate | solution.py:80
  106.7 17.1 %while.41 = (s32[]{:T(128)}, f32[256,256]{1,0:T(8,128)S(1)}, s32[]{:T(128)}, bf16[3,256,8,256]{3,1,2,0:T(8,128)(2,1)S(1)}, s32[3]{0:T(128)}, /*index=5*/bf16[4,8...) while((s32[]{:T(128)}, f32[256,256]{1,0:T(8,128)S(1)}, s32[]{:T(128)}, ...), condition=%wide.region_5.7_spmd, body=%wide.region_4.6_spmd.sunk | while | flops 268500992 | bytes 2621629 | solution.py:55
  107.3 1.3 dynamic_slice.347
  110.5 1.7 fusion.119
  112.8 1.3 dynamic_slice.347
  115.9 1.7 fusion.119
  118.3 1.3 dynamic_slice.347
  121.4 1.7 fusion.119
  123.7 37.8 %reduce-scatter.15.cloned.1.call-done = bf16[32,256]{1,0:T(8,128)(2,1)} async-done(((bf16[256,256]{1,0:T(8,128)(2,1)}), bf16[32,256]{1,0:T(8,128)(2,1)}) %reduce-scatter.15.cloned.1.call-update) | async-done | bytes 16400
  161.6 2.4 multiply_reduce_fusion.2
  164.0 4.6 %collective-permute-done.3 = bf16[1,256,256]{2,1,0:T(8,128)(2,1)S(1)} collective-permute-done((bf16[1,256,256]{2,1,0:T(8,128)(2,1)}, bf16[1,256,256]{2,1,0:T(8,128)(2,1)S(1)}, u32[]{:S(2)}, u32[]{:S(2)}) %collective-permute-start.3) | collective-permute-done | bytes 131104 | tf_op jit(solution)/shard_map/ppermute | solution.py:75
  168.6 1.3 broadcast_multiply_fusion.3
  169.8 3.1 collective-permute-done.4
  173.0 3.5 fusion.25
  176.5 0.8 collective-permute-done.5
  177.4 1.7 fusion.47
  179.5 0.8 copy.18
  180.3 1.8 fusion.97
  182.1 4.6 %pad_maximum_fusion.1 = bf16[4,8,256,256]{3,2,1,0:T(8,128)(2,1)} fusion(bf16[4,1,256,256]{3,2,1,0:T(8,128)(2,1)S(1)} %fusion.97, bf16[4,7,256,256]{3,2,1,0:T(8,128)(2,1)} %fusion.25), kind=kLoop, calls=%fused_computation.31 | loop fusion | flops 2097152 | bytes 8388608 | tf_op jit(solution)/shard_map/concatenate | solution.py:80
  186.8 17.3 %while.42 = (s32[]{:T(128)}, f32[256,256]{1,0:T(8,128)S(1)}, s32[]{:T(128)}, bf16[3,256,8,256]{3,1,2,0:T(8,128)(2,1)S(1)}, s32[3]{0:T(128)}, /*index=5*/bf16[4,8...) while((s32[]{:T(128)}, f32[256,256]{1,0:T(8,128)S(1)}, s32[]{:T(128)}, ...), condition=%wide.region_8.10_spmd, body=%wide.region_7.9_spmd.sunk | while | flops 268500992 | bytes 2621629 | solution.py:55
  187.5 1.2 dynamic_slice.350
  190.6 1.7 fusion.122
  193.0 1.2 dynamic_slice.350
  196.2 1.7 fusion.122
  198.5 1.2 dynamic_slice.350
  201.7 1.7 fusion.122
  204.1 37.2 %reduce-scatter.17.cloned.1.call-done = bf16[32,256]{1,0:T(8,128)(2,1)} async-done(((bf16[256,256]{1,0:T(8,128)(2,1)}), bf16[32,256]{1,0:T(8,128)(2,1)}) %reduce-scatter.17.cloned.1.call-update) | async-done | bytes 16400
  241.3 1.2 multiply_reduce_fusion.1
  242.6 1.2 broadcast_multiply_fusion.2
  243.8 3.2 collective-permute-done.6
  247.0 3.4 fusion.24
  250.4 0.9 collective-permute-done.7
  251.4 0.9 collective-permute-start.8
  252.3 3.5 collective-permute-done.8
  255.8 0.7 copy-done.20
  256.4 0.7 fusion.48
  257.5 0.8 copy.20
  258.3 1.8 fusion.96
  260.1 4.4 %pad_maximum_fusion.2 = bf16[4,8,256,256]{3,2,1,0:T(8,128)(2,1)} fusion(bf16[4,7,256,256]{3,2,1,0:T(8,128)(2,1)} %fusion.24, bf16[4,1,256,256]{3,2,1,0:T(8,128)(2,1)S(1)} %fusion.96), kind=kLoop, calls=%fused_computation.32 | loop fusion | flops 2097152 | bytes 8388608 | tf_op jit(solution)/shard_map/concatenate | solution.py:80
  264.6 15.3 %while.43 = (s32[]{:T(128)}, f32[256,256]{1,0:T(8,128)S(1)}, s32[]{:T(128)}, bf16[3,256,8,256]{3,1,2,0:T(8,128)(2,1)S(1)}, s32[3]{0:T(128)S(1)}, /*index=5*/bf16...) while((s32[]{:T(128)}, f32[256,256]{1,0:T(8,128)S(1)}, s32[]{:T(128)}, ...), condition=%wide.region_11.13_spmd, body=%wide.region_10.12_spmd.sunk | while | flops 268500992 | bytes 2621629 | solution.py:55
  267.8 1.7 fusion.125
  272.7 1.7 fusion.125
  277.6 1.7 fusion.125
  279.9 39.4 %reduce-scatter.19.cloned.1.call-done = bf16[32,256]{1,0:T(8,128)(2,1)} async-done(((bf16[256,256]{1,0:T(8,128)(2,1)}), bf16[32,256]{1,0:T(8,128)(2,1)}) %reduce-scatter.19.cloned.1.call-update) | async-done | bytes 16400
  319.3 1.2 multiply_reduce_fusion
  320.5 1.9 maximum_bitcast_fusion
  322.4 40.1 %all-reduce = (f32[1,256]{1,0:T(1,128)S(1)}, f32[1,256]{1,0:T(1,128)S(1)}, f32[1,256]{1,0:T(1,128)S(1)}, f32[1,256]{1,0:T(1,128)S(1)}) all-reduce(f32[1,256]{1,0:T(1,128)S(1)} %bitcast.252, f32[1,256]{1,0:T(1,128)S(1)} %bitcast.251, f32[1,256]{1,0:T(1,128)S(1)} %bitcast.250, ...), channel_id=1, replica_groups=mesh['row'=4,'col'=8] {'row','col'}, use_global_device_ids=true, to_apply=%region_19.21 | all-reduce | flops 1024 | bytes 8192 | tf_op jit(solution)/shard_map/psum | solution.py:67
  (92 shorter events, 7.1 us)
Async XLA Ops:
  7.2 3.6 copy-start
  7.2 72.6 %reduce-scatter.13.cloned.1.call-start = ((), (), s32[]{:S(2)}) async-start(), calls=%async_computation.4 | async-start | bytes 147456
  10.8 4.3 %copy-start.1 = (bf16[256,1024]{1,0:T(8,128)(2,1)}, bf16[256,1024]{1,0:T(8,128)(2,1)S(1)}, u32[]{:S(2)}) copy-start(bf16[256,1024]{1,0:T(8,128)(2,1)S(1)} %reshape.69) | copy-start | bytes 1572868
  14.0 1.2 copy-start.5
  14.0 3.9 %copy-start.25 = (s32[1,1,3]{2,1,0:T(1,128)S(1)}, s32[1,1,3]{2,1,0:T(1,128)}, u32[]{:S(2)}) copy-start(s32[1,1,3]{2,1,0:T(1,128)} %param.26) | copy-start | bytes 40
  15.2 146.4 %reduce-scatter.15.cloned.1.call-start = ((), (), s32[]{:S(2)}) async-start(), calls=%async_computation.5 | async-start | bytes 147456
  17.9 62.0 %copy-start.15 = (bf16[1,1,256,32]{2,3,1,0:T(8,128)(2,1)S(1)}, bf16[1,1,256,32]{2,3,1,0:T(8,128)(2,1)}, u32[]{:S(2)}) copy-start(bf16[1,1,256,32]{2,3,1,0:T(8,128)(2,1)} %param.23) | copy-start | bytes 49156
  17.9 62.0 %copy-start.21 = (f32[1,1,256]{2,1,0:T(1,128)S(1)}, f32[1,1,256]{2,1,0:T(1,128)}, u32[]{:S(2)}) copy-start(f32[1,1,256]{2,1,0:T(1,128)} %param.21) | copy-start | bytes 3076
  81.6 0.7 copy-start.12
  82.2 4.4 %collective-permute-start = (bf16[1,256,256]{2,1,0:T(8,128)(2,1)S(1)}, bf16[1,256,256]{2,1,0:T(8,128)(2,1)S(1)}, u32[]{:S(2)}, u32[]{:S(2)}) collective-permute-start(bf16[1,256,256]{2,1,0:T(8,128)(2,1)S(1)} %bitcast.236), channel_id=1, source_target_pairs={{0,8},{8,16},{16,24},{24,0},{1,9},{9,17},{17,25},{25,1},{2,10},{10... | collective-permute-start | bytes 393224 | tf_op jit(solution)/shard_map/ppermute | solution.py:75
  82.2 15.0 %copy-start.13 = (bf16[256,256]{1,0:T(8,128)(2,1)S(1)}, bf16[256,256]{1,0:T(8,128)(2,1)}, u32[]{:S(2)}) copy-start(bf16[256,256]{1,0:T(8,128)(2,1)} %copy-done.12) | copy-start | bytes 393220
  86.6 12.4 %copy-start.16 = (bf16[1,256,256]{2,1,0:T(8,128)(2,1)}, bf16[1,256,256]{2,1,0:T(8,128)(2,1)S(1)}, u32[]{:S(2)}) copy-start(bf16[1,256,256]{2,1,0:T(8,128)(2,1)S(1)} %collective-permute-done) | copy-start | bytes 393220
  86.6 4.5 %collective-permute-start.1 = (bf16[1,256,256]{2,1,0:T(8,128)(2,1)S(1)}, bf16[1,256,256]{2,1,0:T(8,128)(2,1)}, u32[]{:S(2)}, u32[]{:S(2)}) collective-permute-start(bf16[1,256,256]{2,1,0:T(8,128)(2,1)S(1)} %collective-permute-done), channel_id=1, source_target_pairs={{0,8},{8,16},{16,24},{24,0},{1,9},{9,17},{17,25},{25,1},{2,10},{10... | collective-permute-start | bytes 393224 | tf_op jit(solution)/shard_map/ppermute | solution.py:75
  91.1 6.1 %collective-permute-start.2 = (bf16[1,256,256]{2,1,0:T(8,128)(2,1)}, bf16[1,256,256]{2,1,0:T(8,128)(2,1)}, u32[]{:S(2)}, u32[]{:S(2)}) collective-permute-start(bf16[1,256,256]{2,1,0:T(8,128)(2,1)} %collective-permute-done.1), channel_id=1, source_target_pairs={{0,8},{8,16},{16,24},{24,0},{1,9},{9,17},{17,25},{25,1},{2,10},{10... | collective-permute-start | bytes 393224 | tf_op jit(solution)/shard_map/ppermute | solution.py:75
  97.2 1.8 copy-start.8
  97.2 1.9 copy-start.2
  100.2 141.1 %reduce-scatter.17.cloned.1.call-start = ((), (), s32[]{:S(2)}) async-start(), calls=%async_computation.6 | async-start | bytes 147456
  102.0 4.6 %copy-start.6 = (bf16[4,1,256,256]{3,2,1,0:T(8,128)(2,1)}, bf16[4,1,256,256]{3,2,1,0:T(8,128)(2,1)S(1)}, u32[]{:S(2)}) copy-start(bf16[4,1,256,256]{3,2,1,0:T(8,128)(2,1)S(1)} %fusion.98) | copy-start | bytes 1572868
  164.0 4.6 %collective-permute-start.3 = (bf16[1,256,256]{2,1,0:T(8,128)(2,1)}, bf16[1,256,256]{2,1,0:T(8,128)(2,1)S(1)}, u32[]{:S(2)}, u32[]{:S(2)}) collective-permute-start(bf16[1,256,256]{2,1,0:T(8,128)(2,1)} %bitcast.38), channel_id=1, source_target_pairs={{0,8},{8,16},{16,24},{24,0},{1,9},{9,17},{17,25},{25,1},{2,10},{10... | collective-permute-start | bytes 393224 | tf_op jit(solution)/shard_map/ppermute | solution.py:75
  164.0 12.5 %copy-start.9 = (bf16[4,7,32,256]{3,2,1,0:T(8,128)(2,1)S(1)}, bf16[4,7,32,256]{3,2,1,0:T(8,128)(2,1)}, u32[]{:S(2)}) copy-start(bf16[4,7,32,256]{3,2,1,0:T(8,128)(2,1)} %slice.40) | copy-start | bytes 1376260
  168.6 4.4 %collective-permute-start.4 = (bf16[1,256,256]{2,1,0:T(8,128)(2,1)S(1)}, bf16[1,256,256]{2,1,0:T(8,128)(2,1)S(1)}, u32[]{:S(2)}, u32[]{:S(2)}) collective-permute-start(bf16[1,256,256]{2,1,0:T(8,128)(2,1)S(1)} %collective-permute-done.3), channel_id=1, source_target_pairs={{0,8},{8,16},{16,24},{24,0},{1,9},{9,17},{17,25},{25,1},{2,10},{10... | collective-permute-start | bytes 393224 | tf_op jit(solution)/shard_map/ppermute | solution.py:75
  173.0 4.4 %copy-start.18 = (bf16[1,256,256]{2,1,0:T(8,128)(2,1)}, bf16[1,256,256]{2,1,0:T(8,128)(2,1)S(1)}, u32[]{:S(2)}) copy-start(bf16[1,256,256]{2,1,0:T(8,128)(2,1)S(1)} %collective-permute-done.4) | copy-start | bytes 393220
  173.0 4.4 %collective-permute-start.5 = (bf16[1,256,256]{2,1,0:T(8,128)(2,1)S(1)}, bf16[1,256,256]{2,1,0:T(8,128)(2,1)S(1)}, u32[]{:S(2)}, u32[]{:S(2)}) collective-permute-start(bf16[1,256,256]{2,1,0:T(8,128)(2,1)S(1)} %collective-permute-done.4), channel_id=1, source_target_pairs={{0,8},{8,16},{16,24},{24,0},{1,9},{9,17},{17,25},{25,1},{2,10},{10... | collective-permute-start | bytes 393224 | tf_op jit(solution)/shard_map/ppermute | solution.py:75
  176.5 2.7 copy-start.3
  176.5 2.5 copy-start.10
  177.4 1.8 copy-start.19
  180.3 139.0 %reduce-scatter.19.cloned.1.call-start = ((), (), s32[]{:S(2)}) async-start(), calls=%async_computation.7 | async-start | bytes 147456
  182.1 4.7 %copy-start.7 = (bf16[4,1,256,256]{3,2,1,0:T(8,128)(2,1)}, bf16[4,1,256,256]{3,2,1,0:T(8,128)(2,1)S(1)}, u32[]{:S(2)}) copy-start(bf16[4,1,256,256]{3,2,1,0:T(8,128)(2,1)S(1)} %fusion.97) | copy-start | bytes 1572868
  241.3 9.1 %copy-start.11 = (bf16[4,7,32,256]{3,2,1,0:T(8,128)(2,1)S(1)}, bf16[4,7,32,256]{3,2,1,0:T(8,128)(2,1)}, u32[]{:S(2)}) copy-start(bf16[4,7,32,256]{3,2,1,0:T(8,128)(2,1)} %copy-done.10) | copy-start | bytes 1376260
  242.5 13.2 %copy-start.14 = (bf16[256,256]{1,0:T(8,128)(2,1)}, bf16[256,256]{1,0:T(8,128)(2,1)S(1)}, u32[]{:S(2)}) copy-start(bf16[256,256]{1,0:T(8,128)(2,1)S(1)} %get-tuple-element.194) | copy-start | bytes 393220
  242.5 4.4 %collective-permute-start.6 = (bf16[1,256,256]{2,1,0:T(8,128)(2,1)S(1)}, bf16[1,256,256]{2,1,0:T(8,128)(2,1)S(1)}, u32[]{:S(2)}, u32[]{:S(2)}) collective-permute-start(bf16[1,256,256]{2,1,0:T(8,128)(2,1)S(1)} %bitcast.240), channel_id=1, source_target_pairs={{0,8},{8,16},{16,24},{24,0},{1,9},{9,17},{17,25},{25,1},{2,10},{10... | collective-permute-start | bytes 393224 | tf_op jit(solution)/shard_map/ppermute | solution.py:75
  247.0 4.4 %collective-permute-start.7 = (bf16[1,256,256]{2,1,0:T(8,128)(2,1)S(1)}, bf16[1,256,256]{2,1,0:T(8,128)(2,1)S(1)}, u32[]{:S(2)}, u32[]{:S(2)}) collective-permute-start(bf16[1,256,256]{2,1,0:T(8,128)(2,1)S(1)} %collective-permute-done.6), channel_id=1, source_target_pairs={{0,8},{8,16},{16,24},{24,0},{1,9},{9,17},{17,25},{25,1},{2,10},{10... | collective-permute-start | bytes 393224 | tf_op jit(solution)/shard_map/ppermute | solution.py:75
  250.4 6.8 %copy-start.4 = (bf16[256,1024]{1,0:T(8,128)(2,1)S(1)}, bf16[256,1024]{1,0:T(8,128)(2,1)}, u32[]{:S(2)}) copy-start(bf16[256,1024]{1,0:T(8,128)(2,1)} %copy-done.1) | copy-start | bytes 1572868
  251.4 5.8 %copy-start.17 = (bf16[1,256,256]{2,1,0:T(8,128)(2,1)}, bf16[1,256,256]{2,1,0:T(8,128)(2,1)S(1)}, u32[]{:S(2)}) copy-start(bf16[1,256,256]{2,1,0:T(8,128)(2,1)S(1)} %collective-permute-done.7) | copy-start | bytes 393220
  251.4 4.4 %collective-permute-start.8 = (bf16[1,256,256]{2,1,0:T(8,128)(2,1)S(1)}, bf16[1,256,256]{2,1,0:T(8,128)(2,1)S(1)}, u32[]{:S(2)}, u32[]{:S(2)}) collective-permute-start(bf16[1,256,256]{2,1,0:T(8,128)(2,1)S(1)} %collective-permute-done.7), channel_id=1, source_target_pairs={{0,8},{8,16},{16,24},{24,0},{1,9},{9,17},{17,25},{25,1},{2,10},{10... | collective-permute-start | bytes 393224 | tf_op jit(solution)/shard_map/ppermute | solution.py:75
  255.8 0.7 copy-start.20
  260.1 4.5 %copy-start.26 = (s32[3]{0:T(128)S(1)}, s32[3]{0:T(128)}, u32[]{:S(2)}) copy-start(s32[3]{0:T(128)} %get-tuple-element.507) | copy-start | bytes 40
  264.6 54.8 %copy-start.22 = (f32[1,1,256]{2,1,0:T(1,128)S(1)}, f32[1,1,256]{2,1,0:T(1,128)}, u32[]{:S(2)}) copy-start(f32[1,1,256]{2,1,0:T(1,128)} %param.21) | copy-start | bytes 3076
  264.6 57.8 %copy-start.23 = (f32[256]{0:T(256)S(1)}, f32[256]{0:T(256)}, u32[]{:S(2)}) copy-start(f32[256]{0:T(256)} %broadcast_multiply_fusion.3) | copy-start | bytes 3076
  264.6 57.8 %copy-start.24 = (f32[256]{0:T(256)S(1)}, f32[256]{0:T(256)}, u32[]{:S(2)}) copy-start(f32[256]{0:T(256)} %broadcast_multiply_fusion.2) | copy-start | bytes 3076
Sparse Core Ops, SparseCore 0:
  15.3 64.5 reduce-scatter.12
  100.3 61.1 reduce-scatter.14
  180.4 60.8 reduce-scatter.16
  258.4 60.8 reduce-scatter.18
